TPU v7x, 256 devices: a 8x8x2 block of a 8x8x16 slice. The times are simulated.
256 devices in a mesh: groups: 2 (over z), ep: 16 (over x, core), tp: 8 (over y).
Axes of the slice: x: 8, y: 8, z: 2, core: 2. Of those that a mesh axis runs over, the one named last changes fastest.
The devices are a block of a 8x8x16 slice.
Arguments:
- tokens: bfloat16 [1024, 7168], P(('groups', 'ep')), parts along dimension 0, may hold values from -6 to 6
- w_gate: bfloat16 [16, 7168, 2048], P('ep', None, 'tp'), may hold values from -0.0625 to 0.0625
- w_up: bfloat16 [16, 7168, 2048], P('ep', None, 'tp'), may hold values from -0.0625 to 0.0625
- w_down: bfloat16 [16, 2048, 7168], P('ep', 'tp'), may hold values from -0.1875 to 0.1875
- router_logits: float32 [1024, 8], P(('groups', 'ep')), parts along dimension 0, may hold values from -6 to 6
- expert_ids: int32 [1024, 8], P(('groups', 'ep')), parts along dimension 0, may hold values from 0 to 15, all different within a row; in each aligned block of 32 rows (0 to 31, 32 to 63, ...) at most 24 rows name the same one
- draft_lengths: int32 [128], P(('groups', 'ep')), parts along dimension 0, may hold values from 7 to 8
- accept_mask: int32 [128, 8], P(('groups', 'ep')), parts along dimension 0, may hold values 0 or 1
Outputs:
- mixed: bfloat16 [1024, 7168], P(('groups', 'ep'), 'tp'), parts along dimension 0
- accepted: int32 [2], P('groups'), parts along dimension 0
There are 2 independent parts, one for each index of `groups`. A program takes and returns all parts, laid end to end along the dimension named above; an argument that names none is the same for every part. Nothing has to cross between parts.
Inputs may be any that keep to these rules, and one draw needn't show every extreme that they name: `expert_ids`: each row names 8 different experts. Among the rows of one ep index (aligned blocks of 32 rows) no expert is named by more than 24 rows, and in every draw some expert is named by exactly 24 rows of some block.
All inputs are finite; a program needn't handle non-finite values. No bound on the sum of `accept_mask` on one device may be relied on, other than what follows from the above.
Results may differ from a plain program's by a relative error of at most 0.017.
Values may be sent and summed in bfloat16 or wider, within the bound.
No kernel may reach another device: no remote copies, remote signals or barrier semaphores. Data moves between devices by JAX's collectives and lax.ppermute only.
A program may use at most 128 MiB of HBM per device.

v0:
```python
import jax
import jax.numpy as jnp
from jax import lax
from jax.sharding import PartitionSpec as P

DRAFT = 8
EXPERTS = 16
CAP = 24


def sent_to_all(array, axis):
    copies = jnp.broadcast_to(array, (lax.axis_size(axis), *array.shape))
    return lax.all_to_all(copies, axis, split_axis=0, concat_axis=0, tiled=True)


def of_everyone(array, axis):
    everything = sent_to_all(array, axis)
    return jnp.sum(everything, axis=0)


def per_device(tokens, w_gate, w_up, w_down, router_logits, expert_ids, draft_lengths, accept_mask):
    tok_rows = tokens.shape[0]
    width = tokens.shape[1]
    top = expert_ids.shape[1]
    tp_count = lax.axis_size("tp")
    slice_width = width // tp_count
    live = jnp.arange(DRAFT, dtype=jnp.int32)[None, :] < draft_lengths[:, None]
    live_rows = live.reshape(tok_rows)
    live_tokens = jnp.where(live_rows[:, None], tokens, jnp.zeros((), tokens.dtype))
    sig = jax.nn.sigmoid(router_logits)
    gates = 2.827 * sig / jnp.sum(sig, axis=1, keepdims=True)
    flat_ids = expert_ids.reshape(-1)
    onehot = (flat_ids[:, None] == jnp.arange(EXPERTS, dtype=jnp.int32)[None, :]).astype(jnp.int32)
    rank = jnp.cumsum(onehot, axis=0) - 1
    slot = jnp.sum(rank * onehot, axis=1)
    target = flat_ids * CAP + slot
    source = jnp.arange(tok_rows * top, dtype=jnp.int32) // top
    own_cols = lax.dynamic_slice_in_dim(
        live_tokens, lax.axis_index("tp") * slice_width, slice_width, 1
    )
    sendbuf = jnp.zeros((EXPERTS * CAP, slice_width), tokens.dtype).at[target].set(own_cols[source])
    received = lax.all_to_all(
        sendbuf.reshape(EXPERTS, CAP, slice_width), "ep", split_axis=0, concat_axis=1, tiled=True
    )
    piece = lax.all_gather(received, "tp", axis=2, tiled=True)
    gate_sum = jnp.einsum("emd,edf->emf", piece, w_gate, preferred_element_type=jnp.float32)
    up_sum = jnp.einsum("emd,edf->emf", piece, w_up, preferred_element_type=jnp.float32)
    hidden = (jax.nn.silu(gate_sum) * up_sum).astype(jnp.bfloat16)
    partial_value = jnp.einsum("emf,efd->emd", hidden, w_down, preferred_element_type=jnp.float32)
    expert_out = lax.psum_scatter(
        partial_value.astype(jnp.bfloat16), "tp", scatter_dimension=2, tiled=True
    )
    returned = lax.all_to_all(expert_out, "ep", split_axis=1, concat_axis=0, tiled=True)
    flat_back = returned.reshape(EXPERTS * CAP, returned.shape[2])
    picked = flat_back[target].reshape(tok_rows, top, returned.shape[2])
    mixed = jnp.sum(gates[:, :, None] * picked.astype(jnp.float32), axis=1).astype(jnp.bfloat16)
    passed = accept_mask * live.astype(jnp.int32)
    prefix = jnp.cumprod(passed, axis=1)
    local_count = jnp.sum(prefix)
    total = of_everyone(local_count, "ep")
    accepted = total.reshape(1)
    return (mixed, accepted)


def solution(mesh):
    placed = (
        P(("groups", "ep"), None),
        P("ep", None, "tp"),
        P("ep", None, "tp"),
        P("ep", "tp", None),
        P(("groups", "ep"), None),
        P(("groups", "ep"), None),
        P(("groups", "ep")),
        P(("groups", "ep"), None),
    )
    return jax.shard_map(
        per_device,
        mesh=mesh,
        in_specs=placed,
        out_specs=(P(("groups", "ep"), "tp"), P("groups")),
        check_vma=False,
    )
```

profile of v0, /device:TPU:513, one launch (start us, length us, event | category | flops | bytes accessed | tf_op | source)
XLA Modules:
  0.0 286.3 jit_solution(15594155464627464665)
XLA Ops:
  7.2 0.8 copy.36
  8.2 0.7 broadcast_multiply_fusion
  8.9 0.6 reduce-window.6
  9.9 0.7 iota_compare_fusion.2
  10.8 0.9 dynamic-slice_select_fusion
  11.7 3.5 %scatter_custom_fusion = bf16[384,896]{1,0:T(8,128)(2,1)S(1)} fusion(s32[256]{0:T(256)S(1)} %bitcast.67, bf16[32,896]{1,0:T(8,128)(2,1)S(1)} %dynamic-slice_select_fusion, s32[1024]{0:T(1024)S(1)} %pad_clamp_fusion.1, bf16[]{:T(256)} %constant.43.clone.1), kind=kCustom, calls=%fused_computation.19 | custom fusion | bytes 688130 | tf_op jit(solution)/shard_map/scatter | solution.py:41
  15.2 44.7 %all_to_all.27 = bf16[16,24,896]{2,1,0:T(8,128)(2,1)} all-to-all(bf16[16,24,896]{2,1,0:T(8,128)(2,1)S(1)} %bitcast.66), channel_id=1, replica_groups=mesh['groups'=2,'ep'=16,'tp'=8] {'ep'}, dimensions={0} | all-to-all | bytes 1376256 | tf_op jit(solution)/shard_map/all_to_all | solution.py:42
  60.1 66.0 %all-gather.2.cloned.1.call-done = bf16[1,384,7168]{2,1,0:T(8,128)(2,1)} async-done(((bf16[1,384,896]{2,1,0:T(8,128)(2,1)}), bf16[1,384,7168]{2,1,0:T(8,128)(2,1)}) %all-gather.2.cloned.1.call-update) | async-done | bytes 5505040 | tf_op jit(solution)/shard_map/all_gather | solution.py:45
  126.1 5.4 %fusion.3 = f32[384,256]{1,0:T(8,128)S(1)} fusion(bf16[1,384,7168]{2,1,0:T(8,128)(2,1)} %all-gather.2.cloned.1.call-done, bf16[1,7168,256]{2,1,0:T(8,128)(2,1)} %param.9), kind=kOutput, calls=%fused_computation.8 | convolution fusion | flops 1409286144 | bytes 9568256 | tf_op jit(solution)/shard_map/emd,edf->emf/dot_general | solution.py:46
  131.5 0.9 copy-done.5
  132.4 1.6 fusion.13
  134.0 0.4 copy-done
  134.4 4.0 %fusion = bf16[1,384,7168]{2,1,0:T(8,128)(2,1)} fusion(bf16[384,256]{1,0:T(8,128)(2,1)S(1)} %fusion.13, bf16[1,256,7168]{2,1,0:T(8,128)(2,1)S(1)} %copy-done), kind=kOutput, calls=%fused_computation.4 | convolution fusion | flops 1412038656 | bytes 9371648 | tf_op jit(solution)/shard_map/emf,efd->emd/dot_general | solution.py:49
  138.4 24.0 %copy.41 = bf16[1,384,7168]{1,0,2:T(2,128)(2,1)} copy(bf16[1,384,7168]{2,1,0:T(8,128)(2,1)} %fusion) | data formatting | bytes 11010048
  162.4 7.4 %copy.51 = bf16[7168,1,384]{2,0,1:T(8,128)(2,1)} copy(bf16[7168,1,384]{2,1,0:T(2,128)(2,1)} %bitcast.60) | data formatting | bytes 11010048
  169.9 0.6 copy-done.2
  170.6 0.2 reduce_window.9
  170.8 0.6 reduce_sum.51
  171.4 1.2 broadcast_in_dim.29
  172.6 7.6 %all-to-all-start.2 = ((s32[16,1,1]{2,1,0:T(1,128)}), s32[16,1,1]{2,1,0:T(1,128)S(1)}, u32[]{:S(2)}, u32[]{:S(2)}) async-start(s32[16,1,1]{2,1,0:T(1,128)} %broadcast_in_dim.29), calls=%async_computation.2 | async-start | bytes 16384 | tf_op jit(solution)/shard_map/all_to_all | solution.py:13
  180.2 57.8 %reduce-scatter.4.cloned.1.call-done = bf16[896,384]{1,0:T(8,128)(2,1)} async-done(((bf16[7168,384]{1,0:T(8,128)(2,1)}), bf16[896,384]{1,0:T(8,128)(2,1)}) %reduce-scatter.4.cloned.1.call-update) | async-done | bytes 688144
  238.0 1.8 reshape_bitcast_fusion
  239.8 2.3 copy.39
  242.1 0.5 broadcast.160
  242.6 4.8 %reduce.3 = bf16[384,896]{1,0:T(8,128)(2,1)S(1)} reduce(bf16[384,1,896]{2,1,0:T(2,128)(2,1)S(1)} %bitcast.63, bf16[]{:T(256)} %broadcast.160), dimensions={1}, to_apply=%bitcast.54.reduce_sub_computation | reduce | bytes 1376258
  247.5 1.0 reshape.202
  248.5 7.4 %all-to-all-start.1 = ((bf16[16,2,10752]{2,1,0:T(2,128)(2,1)}), bf16[16,2,10752]{2,1,0:T(2,128)(2,1)S(1)}, u32[]{:S(2)}, u32[]{:S(2)}) async-start(bf16[16,2,10752]{2,1,0:T(2,128)(2,1)} %reshape.202), calls=%async_computation.1 | async-start | bytes 1376256 | tf_op jit(solution)/shard_map/all_to_all | solution.py:53
  256.1 0.7 reduce_sum.52
  256.7 19.8 %all-to-all-done.1 = bf16[16,2,10752]{2,1,0:T(2,128)(2,1)S(1)} async-done(((bf16[16,2,10752]{2,1,0:T(2,128)(2,1)}), bf16[16,2,10752]{2,1,0:T(2,128)(2,1)S(1)}, u32[]{:S(2)}, u32[]{:S(2)}) %all-to-all-start.1) | async-done | bytes 688160 | tf_op jit(solution)/shard_map/all_to_all | solution.py:53
  276.6 0.6 reshape.203
  277.2 1.2 gather_fusion
  278.4 1.0 fusion.18
  (33 shorter events, 1.3 us)
Async XLA Ops:
  7.2 118.9 %all-gather.2.cloned.1.call-start = ((), (), s32[]{:S(2)}) async-start(), calls=%async_computation.4 | async-start | bytes 6193152 | tf_op jit(solution)/shard_map/all_gather | solution.py:45
  60.0 178.0 %reduce-scatter.4.cloned.1.call-start = ((), (), s32[]{:S(2)}) async-start(), calls=%async_computation.5 | async-start | bytes 6193152
  126.1 5.4 %copy-start.4 = (bf16[1,384,7168]{2,1,0:T(8,128)(2,1)S(1)}, bf16[1,384,7168]{2,1,0:T(8,128)(2,1)}, u32[]{:S(2)}) copy-start(bf16[1,384,7168]{2,1,0:T(8,128)(2,1)} %all-gather.2.cloned.1.call-done) | copy-start | bytes 16515076
  126.1 6.3 %copy-start.5 = (bf16[1,7168,256]{2,1,0:T(8,128)(2,1)S(1)}, bf16[1,7168,256]{2,1,0:T(8,128)(2,1)}, u32[]{:S(2)}) copy-start(bf16[1,7168,256]{2,1,0:T(8,128)(2,1)} %param.10) | copy-start | bytes 11010052
  132.4 2.0 copy-start
  169.8 0.7 copy-start.2
  169.8 0.7 copy-start.3
  172.6 75.9 %all-to-all-start.2 = ((s32[16,1,1]{2,1,0:T(1,128)}), s32[16,1,1]{2,1,0:T(1,128)S(1)}, u32[]{:S(2)}, u32[]{:S(2)}) async-start(s32[16,1,1]{2,1,0:T(1,128)} %broadcast_in_dim.29), calls=%async_computation.2 | async-start | bytes 16384 | tf_op jit(solution)/shard_map/all_to_all | solution.py:13
  239.8 16.2 %copy-start.1 = (f32[32,8]{0,1:T(8,128)S(1)}, f32[32,8]{0,1:T(8,128)}, u32[]{:S(2)}) copy-start(f32[32,8]{0,1:T(8,128)} %param.12) | copy-start | bytes 3076
  248.5 28.1 %all-to-all-start.1 = ((bf16[16,2,10752]{2,1,0:T(2,128)(2,1)}), bf16[16,2,10752]{2,1,0:T(2,128)(2,1)S(1)}, u32[]{:S(2)}, u32[]{:S(2)}) async-start(bf16[16,2,10752]{2,1,0:T(2,128)(2,1)} %reshape.202), calls=%async_computation.1 | async-start | bytes 1376256 | tf_op jit(solution)/shard_map/all_to_all | solution.py:53
Sparse Core Ops, SparseCore 0:
  60.1 65.8 all-gather.1
  170.0 67.9 reduce-scatter.3
where the time goes:
time: 288 us; the launch traced here: 286 us
  waiting for transfers between devices  144 us (50%)
  local copies, waits for them, and re-layouts  47.2 us (16%)
  blocking collectives  44.7 us (16%)
  starting transfers between devices  15.1 us (5%)
  between operations  14.2 us (5%)
  matrix products  10.9 us (4%)
  other arithmetic  10.4 us (4%)
    all_gather x1, waiting for transfers between devices, per_device(): piece = lax.all_gather(received, 'tp', axis=2, tiled=True)  66 us
    unnamed x3, waiting for transfers between devices  57.9 us
    all_to_all x1, blocking collectives, per_device(): lax.all_to_all(sendbuf.reshape(EXPERTS, CAP, slice_width), 'ep', split_ax...  44.7 us
    unnamed x20, local copies, waits for them, and re-layouts  38.2 us
    all_to_all x1, waiting for transfers between devices, per_device(): lax.all_to_all(expert_out, 'ep', split_axis=1, concat_axis=0, tiled=True)  19.8 us
    all_to_all x1, starting transfers between devices, sent_to_all(): return lax.all_to_all(copies, axis, split_axis=0, concat_axis=0, tiled=True)  7.55 us
    all_to_all x1, starting transfers between devices, per_device(): lax.all_to_all(expert_out, 'ep', split_axis=1, concat_axis=0, tiled=True)  7.44 us
  transfers between devices with their start and end apart: 4, of which 3 were waited for; matrix products, arithmetic and copies ran while one was open for 5% of the time, Pallas kernels for 0%

commit v1 on v0

--- a/solution.py
+++ b/solution.py
@@ -42,7 +42,9 @@
     received = lax.all_to_all(
         sendbuf.reshape(EXPERTS, CAP, slice_width), "ep", split_axis=0, concat_axis=1, tiled=True
     )
-    piece = lax.all_gather(received, "tp", axis=2, tiled=True)
+    piece = jnp.concatenate(
+        lax.all_to_all(jnp.stack([received] * lax.axis_size("tp")), "tp", 0, 0), axis=2
+    )
     gate_sum = jnp.einsum("emd,edf->emf", piece, w_gate, preferred_element_type=jnp.float32)
     up_sum = jnp.einsum("emd,edf->emf", piece, w_up, preferred_element_type=jnp.float32)
     hidden = (jax.nn.silu(gate_sum) * up_sum).astype(jnp.bfloat16)

time: 288 us -> 352 us (1.22)
  blocking collectives: 44.7 us -> 172 us
  waiting for transfers between devices: 144 us -> 79 us
  matrix products: 10.9 us -> 14.6 us
  starting transfers between devices: 15.1 us -> 11.4 us
    all_to_all x0 -> x1, blocking collectives: none -> 128 us  [per_device(): lax.all_to_all(jnp.stack([received] * lax.axis_size('tp')), 'tp', 0, 0)]
    all_gather x1 -> x0, waiting for transfers between devices: 66 us -> none  [per_device(): piece = lax.all_gather(received, 'tp', axis=2, tiled=True)]
    dot_general x1, matrix products: 3.96 us -> 13 us  [per_device(): jnp.einsum('emf,efd->emd', hidden, w_down, preferred_element_type=jnp.flo...]
    dot_general x1, matrix products: 5.39 us -> 1.62 us  [per_device(): jnp.einsum('emd,edf->emf', piece, w_gate, preferred_element_type=jnp.floa...]
    all_to_all x1, starting transfers between devices: 7.55 us -> 3.85 us  [sent_to_all(): return lax.all_to_all(copies, axis, split_axis=0, concat_axis=0, tiled=True)]
    unnamed x3 -> x2, waiting for transfers between devices: 57.9 us -> 59.2 us
    unnamed x20 -> x18, local copies, waits for them, and re-layouts: 38.2 us -> 39.2 us
  transfers between devices with their start and end apart: 4 -> 3, of which waited for: 3 -> 2; matrix products, arithmetic and copies ran while one was open for 5% -> 4% of each run, Pallas kernels for 0% -> 0%
where the time goes in v1:
time: 352 us; the launch traced here: 351 us
  blocking collectives  172 us (49%)
  waiting for transfers between devices  79 us (22%)
  local copies, waits for them, and re-layouts  49 us (14%)
  matrix products  14.6 us (4%)
  between operations  14.2 us (4%)
  starting transfers between devices  11.4 us (3%)
  other arithmetic  10.4 us (3%)
    all_to_all x1, blocking collectives, per_device(): lax.all_to_all(jnp.stack([received] * lax.axis_size('tp')), 'tp', 0, 0)  128 us
    unnamed x2, waiting for transfers between devices  59.2 us
    all_to_all x1, blocking collectives, per_device(): lax.all_to_all(sendbuf.reshape(EXPERTS, CAP, slice_width), 'ep', split_ax...  44 us
    unnamed x18, local copies, waits for them, and re-layouts  39.2 us
    all_to_all x1, waiting for transfers between devices, per_device(): lax.all_to_all(expert_out, 'ep', split_axis=1, concat_axis=0, tiled=True)  19.8 us
    dot_general x1, matrix products, per_device(): jnp.einsum('emf,efd->emd', hidden, w_down, preferred_element_type=jnp.flo...  13 us
    all_to_all x1, starting transfers between devices, per_device(): lax.all_to_all(expert_out, 'ep', split_axis=1, concat_axis=0, tiled=True)  7.46 us
  transfers between devices with their start and end apart: 3, of which 2 were waited for; matrix products, arithmetic and copies ran while one was open for 4% of the time, Pallas kernels for 0%

profile of v1, /device:TPU:513, one launch (start us, length us, event | category | flops | bytes accessed | tf_op | source)
XLA Modules:
  0.0 350.7 jit_solution(2645427229953750391)
XLA Ops:
  7.2 0.8 copy.48
  8.2 0.7 broadcast_multiply_fusion
  8.9 0.6 reduce-window.6
  9.9 0.7 iota_compare_fusion.2
  10.8 0.9 dynamic-slice_select_fusion
  11.7 3.5 scatter_custom_fusion
  15.2 44.0 %all_to_all.29 = bf16[16,24,896]{2,1,0:T(8,128)(2,1)S(1)} all-to-all(bf16[16,24,896]{2,1,0:T(8,128)(2,1)S(1)} %bitcast.73), channel_id=1, replica_groups=mesh['groups'=2,'ep'=16,'tp'=8] {'ep'}, dimensions={0} | all-to-all | bytes 1376256 | tf_op jit(solution)/shard_map/all_to_all | solution.py:42
  59.2 0.4 copy.51
  59.6 0.5 stack.5
  60.1 128.1 %all_to_all.30 = bf16[8,1,384,896]{2,3,1,0:T(8,128)(2,1)S(1)} all-to-all(bf16[8,1,384,896]{2,3,1,0:T(8,128)(2,1)S(1)} %stack.5), channel_id=1, replica_groups=mesh['groups'=2,'ep'=16,'tp'=8] {'tp'}, dimensions={0} | all-to-all | bytes 11010048 | tf_op jit(solution)/shard_map/all_to_all | solution.py:46
  188.2 2.4 copy-done
  190.6 1.6 fusion.4
  192.2 13.0 %fusion = bf16[1,384,7168]{2,1,0:T(8,128)(2,1)} fusion(bf16[1,256,7168]{2,1,0:T(8,128)(2,1)} %param.11, bf16[384,7168]{0,1:T(8,128)(2,1)} %bitcast.67, bf16[1,7168,256]{2,1,0:T(8,128)(2,1)} %param.10, f32[384,256]{1,0:T(8,128)S(1)} %fusion.4), kind=kOutput, calls=%fused_computation.4 | convolution fusion | flops 2821914624 | bytes 18743296 | tf_op jit(solution)/shard_map/emf,efd->emd/dot_general | solution.py:51
  205.2 24.0 %copy.55 = bf16[1,384,7168]{1,0,2:T(2,128)(2,1)} copy(bf16[1,384,7168]{2,1,0:T(8,128)(2,1)} %fusion) | data formatting | bytes 11010048
  229.2 7.4 %copy.65 = bf16[7168,1,384]{2,0,1:T(8,128)(2,1)} copy(bf16[7168,1,384]{2,1,0:T(2,128)(2,1)} %bitcast.68) | data formatting | bytes 11010048
  236.7 0.6 copy-done.3
  237.4 0.2 reduce_window.9
  237.5 0.6 reduce_sum.51
  238.2 1.2 broadcast_in_dim.29
  239.4 3.9 %all-to-all-start.3 = ((s32[16,1,1]{2,1,0:T(1,128)}), s32[16,1,1]{2,1,0:T(1,128)S(1)}, u32[]{:S(2)}, u32[]{:S(2)}) async-start(s32[16,1,1]{2,1,0:T(1,128)} %broadcast_in_dim.29), calls=%async_computation.3 | async-start | bytes 16384 | tf_op jit(solution)/shard_map/all_to_all | solution.py:13
  243.3 59.1 %reduce-scatter.4.cloned.1.call-done = bf16[896,384]{1,0:T(8,128)(2,1)} async-done(((bf16[7168,384]{1,0:T(8,128)(2,1)}), bf16[896,384]{1,0:T(8,128)(2,1)}) %reduce-scatter.4.cloned.1.call-update) | async-done | bytes 688144
  302.4 1.8 reshape_bitcast_fusion
  304.2 2.3 copy.53
  306.6 0.5 broadcast.162
  307.1 4.8 %reduce.3 = bf16[384,896]{1,0:T(8,128)(2,1)S(1)} reduce(bf16[384,1,896]{2,1,0:T(2,128)(2,1)S(1)} %bitcast.71, bf16[]{:T(256)} %broadcast.162), dimensions={1}, to_apply=%bitcast.50.reduce_sub_computation | reduce | bytes 1376258
  311.9 1.0 reshape.214
  312.9 7.5 %all-to-all-start.2 = ((bf16[16,2,10752]{2,1,0:T(2,128)(2,1)}), bf16[16,2,10752]{2,1,0:T(2,128)(2,1)S(1)}, u32[]{:S(2)}, u32[]{:S(2)}) async-start(bf16[16,2,10752]{2,1,0:T(2,128)(2,1)} %reshape.214), calls=%async_computation.2 | async-start | bytes 1376256 | tf_op jit(solution)/shard_map/all_to_all | solution.py:55
  320.5 0.7 reduce_sum.52
  321.2 19.8 %all-to-all-done.2 = bf16[16,2,10752]{2,1,0:T(2,128)(2,1)S(1)} async-done(((bf16[16,2,10752]{2,1,0:T(2,128)(2,1)}), bf16[16,2,10752]{2,1,0:T(2,128)(2,1)S(1)}, u32[]{:S(2)}, u32[]{:S(2)}) %all-to-all-start.2) | async-done | bytes 688160 | tf_op jit(solution)/shard_map/all_to_all | solution.py:55
  341.0 0.6 reshape.215
  341.7 1.2 gather_fusion
  342.9 1.0 fusion.12
  (30 shorter events, 1.2 us)
Async XLA Ops:
  7.2 295.2 %reduce-scatter.4.cloned.1.call-start = ((), (), s32[]{:S(2)}) async-start(), calls=%async_computation.5 | async-start | bytes 6193152
  60.1 130.5 %copy-start.1 = (bf16[1,7168,256]{2,1,0:T(8,128)(2,1)S(1)}, bf16[1,7168,256]{2,1,0:T(8,128)(2,1)}, u32[]{:S(2)}) copy-start(bf16[1,7168,256]{2,1,0:T(8,128)(2,1)} %param.9) | copy-start | bytes 11010052
  188.2 2.4 copy-start
  236.6 0.7 copy-start.3
  236.6 0.7 copy-start.4
  239.4 73.5 %all-to-all-start.3 = ((s32[16,1,1]{2,1,0:T(1,128)}), s32[16,1,1]{2,1,0:T(1,128)S(1)}, u32[]{:S(2)}, u32[]{:S(2)}) async-start(s32[16,1,1]{2,1,0:T(1,128)} %broadcast_in_dim.29), calls=%async_computation.3 | async-start | bytes 16384 | tf_op jit(solution)/shard_map/all_to_all | solution.py:13
  304.2 16.2 %copy-start.2 = (f32[32,8]{0,1:T(8,128)S(1)}, f32[32,8]{0,1:T(8,128)}, u32[]{:S(2)}) copy-start(f32[32,8]{0,1:T(8,128)} %param.12) | copy-start | bytes 3076
  312.9 28.1 %all-to-all-start.2 = ((bf16[16,2,10752]{2,1,0:T(2,128)(2,1)}), bf16[16,2,10752]{2,1,0:T(2,128)(2,1)S(1)}, u32[]{:S(2)}, u32[]{:S(2)}) async-start(bf16[16,2,10752]{2,1,0:T(2,128)(2,1)} %reshape.214), calls=%async_computation.2 | async-start | bytes 1376256 | tf_op jit(solution)/shard_map/all_to_all | solution.py:55
Sparse Core Ops, SparseCore 0:
  236.8 65.5 reduce-scatter.3
